TPU v7x, 32 devices: a whole 2x2x4 slice. The times are simulated.
32 devices in a mesh: gx: 4 (over x, core), gy: 4 (over z), gz: 2 (over y).
Axes of the slice: x: 2, y: 2, z: 4, core: 2. Of those that a mesh axis runs over, the one named last changes fastest.
Arguments:
- outcomes: bfloat16 [24576, 2048], P(('gx', 'gy', 'gz')), may hold values from -6 to 6
- sketch: bfloat16 [24576, 128], P(('gx', 'gy', 'gz')), may hold values from -6 to 6
Outputs:
- left_basis: float32 [24576, 128], P(('gx', 'gy', 'gz'))
- factor: float32 [128, 128], replicated
All inputs are finite; a program needn't handle non-finite values.
Results may differ from a plain program's by a relative error of at most 0.005.
Values may be sent and summed in bfloat16 or wider, within the bound.
A program may use at most 64 MiB of HBM per device.

v0:
```python
import math
import jax
import jax.numpy as jnp
from jax import lax
from jax.sharding import PartitionSpec as P

POWER = 2


def per_device(outcomes, sketch):
    device_count = lax.axis_size(("gx", "gy", "gz"))
    rows_here = outcomes.shape[0]
    day_count = outcomes.shape[1]
    unit_count = rows_here * device_count
    current = sketch
    left_basis = None
    lower_tri = None
    for power_step in range(POWER):
        partial_sum = lax.dot_general(
            outcomes, current, (((0,), (0,)), ((), ())), preferred_element_type=jnp.float32
        )
        summed = lax.psum(partial_sum, ("gx", "gy", "gz"))
        day_weights = (summed / math.sqrt(unit_count)).astype(jnp.bfloat16)
        projected = jnp.dot(outcomes, day_weights, preferred_element_type=jnp.float32)
        projected = projected / math.sqrt(day_count)
        gram_local = jnp.dot(projected.T, projected, precision=lax.Precision.HIGHEST) / unit_count
        gram = lax.psum(gram_local, ("gx", "gy", "gz"))
        lower_tri = jnp.linalg.cholesky(gram)
        left_basis = lax.linalg.triangular_solve(
            lower_tri, projected, left_side=False, lower=True, transpose_a=True
        )
        current = left_basis.astype(jnp.bfloat16)
    return (left_basis, lower_tri.T)


def solution(mesh):
    return jax.shard_map(
        per_device,
        mesh=mesh,
        in_specs=(P(("gx", "gy", "gz"), None), P(("gx", "gy", "gz"), None)),
        out_specs=(P(("gx", "gy", "gz"), None), P()),
        check_vma=False,
    )
```

profile of v0, /device:TPU:1, one launch (start us, length us, event | category | flops | bytes accessed | tf_op | source)
XLA Modules:
  0.0 607.3 jit_solution(11905937048318065328)
XLA Ops:
  7.2 1.8 copy-done
  9.1 3.0 fusion.16
  12.1 133.1 %all-reduce.5.cloned.1.call-done = f32[2048,128]{1,0:T(8,128)} async-done(((f32[2048,128]{1,0:T(8,128)}), f32[2048,128]{1,0:T(8,128)}) %all-reduce.5.cloned.1.call-update) | async-done | bytes 1048592 | tf_op jit(solution)/shard_map/psum | solution.py:22
  145.2 2.4 convolution_multiply_fusion.1
  147.6 1.1 convolution_multiply_fusion.3
  148.8 123.7 %all-reduce.7.cloned.1.call-done = f32[128,128]{0,1:T(8,128)} async-done(((f32[128,128]{0,1:T(8,128)}), f32[128,128]{0,1:T(8,128)}) %all-reduce.7.cloned.1.call-update) | async-done | bytes 65552 | tf_op jit(solution)/shard_map/psum | solution.py:27
  272.5 1.6 copy.5
  274.0 1.5 fusion.9
  275.5 13.2 %cholesky.44 = f32[128,128]{1,0:T(8,128)} custom-call(f32[128,128]{1,0:T(8,128)} %fusion.9), custom_call_target="Cholesky" | custom-call | tf_op jit(solution)/shard_map/jit(cholesky)/cholesky | solution.py:28
  290.2 2.1 fusion.5
  292.4 11.3 %custom-call.6 = f32[1,128,128]{1,2,0:T(8,128)} custom-call(f32[1,128,128]{2,1,0:T(8,128)} %fusion.5), custom_call_target="InvertDiagBlocksLowerTriangular" | custom-call | tf_op jit(solution)/shard_map/triangular_solve/custom-call.0 | solution.py:29
  303.6 1.3 fusion
  305.0 2.4 convolution_bitcast_fusion
  307.6 129.2 %all-reduce.9.cloned.1.call-done = f32[2048,128]{1,0:T(8,128)} async-done(((f32[2048,128]{1,0:T(8,128)}), f32[2048,128]{1,0:T(8,128)}) %all-reduce.9.cloned.1.call-update) | async-done | bytes 1048592 | tf_op jit(solution)/shard_map/psum | solution.py:22
  436.8 2.4 convolution_multiply_fusion
  440.4 123.6 %all-reduce.11.cloned.1.call-done = f32[128,128]{0,1:T(8,128)} async-done(((f32[128,128]{0,1:T(8,128)}), f32[128,128]{0,1:T(8,128)}) %all-reduce.11.cloned.1.call-update) | async-done | bytes 65552 | tf_op jit(solution)/shard_map/psum | solution.py:27
  564.0 1.6 copy.7
  565.5 1.5 fusion.7
  567.0 13.2 %cholesky.55 = f32[128,128]{1,0:T(8,128)} custom-call(f32[128,128]{1,0:T(8,128)} %fusion.7), custom_call_target="Cholesky" | custom-call | tf_op jit(solution)/shard_map/jit(cholesky)/cholesky | solution.py:28
  581.7 2.1 fusion.13
  583.9 1.6 copy.9
  585.4 11.3 %custom-call.7 = f32[1,128,128]{1,2,0:T(8,128)} custom-call(f32[1,128,128]{2,1,0:T(8,128)} %get-tuple-element.7), custom_call_target="InvertDiagBlocksLowerTriangular" | custom-call | tf_op jit(solution)/shard_map/triangular_solve/custom-call.0 | solution.py:29
  596.7 2.1 convolution_bitcast_fusion.1
  598.8 1.9 copy.8
  (14 shorter events, 4.5 us)
Async XLA Ops:
  7.2 1.9 copy-start
  7.2 138.0 %all-reduce.5.cloned.1.call-start = ((), (), s32[]{:S(2)}) async-start(), calls=%async_computation | async-start | bytes 2097152 | tf_op jit(solution)/shard_map/psum | solution.py:22
  12.1 260.4 %all-reduce.7.cloned.1.call-start = ((), (), s32[]{:S(2)}) async-start(), calls=%async_computation.1 | async-start | bytes 131072 | tf_op jit(solution)/shard_map/psum | solution.py:27
  148.7 288.1 %all-reduce.9.cloned.1.call-start = ((), (), s32[]{:S(2)}) async-start(), calls=%async_computation.2 | async-start | bytes 2097152 | tf_op jit(solution)/shard_map/psum | solution.py:22
  307.4 256.6 %all-reduce.11.cloned.1.call-start = ((), (), s32[]{:S(2)}) async-start(), calls=%async_computation.3 | async-start | bytes 131072 | tf_op jit(solution)/shard_map/psum | solution.py:27
Sparse Core Ops, SparseCore 0:
  13.2 131.9 all-reduce.4
  151.3 121.1 all-reduce.6
  307.5 129.2 all-reduce.8
  442.8 121.1 all-reduce.10
where the time goes:
time: 608 us; the launch traced here: 607 us
  waiting for transfers between devices  510 us (84%)
  other arithmetic  59.2 us (10%)
  matrix products  15.8 us (3%)
  between operations  13.8 us (2%)
  local copies, waits for them, and re-layouts  8.45 us (1%)
    psum x2, waiting for transfers between devices, per_device(): summed = lax.psum(partial_sum, ('gx', 'gy', 'gz'))  262 us
    psum x2, waiting for transfers between devices, per_device(): gram = lax.psum(gram_local, ('gx', 'gy', 'gz'))  247 us
    another operation x6, other arithmetic, per_device(): lower_tri = jnp.linalg.cholesky(gram)  29.4 us
    another operation x3, other arithmetic, per_device(): lax.linalg.triangular_solve(lower_tri, projected, left_side=False, lower=...  24.7 us
  transfers between devices with their start and end apart: 4, of which 4 were waited for; matrix products, arithmetic and copies ran while one was open for 0% of the time, Pallas kernels for 0%

commit v1 on v0

--- a/solution.py
+++ b/solution.py
@@ -24,7 +24,12 @@
         projected = jnp.dot(outcomes, day_weights, preferred_element_type=jnp.float32)
         projected = projected / math.sqrt(day_count)
         gram_local = jnp.dot(projected.T, projected, precision=lax.Precision.HIGHEST) / unit_count
-        gram = lax.psum(gram_local, ("gx", "gy", "gz"))
+
+        def mix_frame(patch):
+            view_out = jax.lax.all_gather(patch, ("gx", "gy", "gz"))
+            return jnp.sum(view_out, 0)
+
+        gram = mix_frame(gram_local)
         lower_tri = jnp.linalg.cholesky(gram)
         left_basis = lax.linalg.triangular_solve(
             lower_tri, projected, left_side=False, lower=True, transpose_a=True

time: 608 us -> 478 us (0.79)
  waiting for transfers between devices: 510 us -> 375 us
    psum x2 -> x0, waiting for transfers between devices: 247 us -> none  [per_device(): gram = lax.psum(gram_local, ('gx', 'gy', 'gz'))]
    all_gather x0 -> x2, waiting for transfers between devices: none -> 113 us  [mix_frame(): view_out = jax.lax.all_gather(patch, ('gx', 'gy', 'gz'))]
where the time goes in v1:
time: 478 us; the launch traced here: 477 us
  waiting for transfers between devices  375 us (78%)
  other arithmetic  63.9 us (13%)
  matrix products  15.8 us (3%)
  between operations  13.8 us (3%)
  local copies, waits for them, and re-layouts  8.45 us (2%)
    psum x2, waiting for transfers between devices, per_device(): summed = lax.psum(partial_sum, ('gx', 'gy', 'gz'))  261 us
    all_gather x2, waiting for transfers between devices, mix_frame(): view_out = jax.lax.all_gather(patch, ('gx', 'gy', 'gz'))  113 us
    another operation x6, other arithmetic, per_device(): lower_tri = jnp.linalg.cholesky(gram)  29.4 us
    another operation x3, other arithmetic, per_device(): lax.linalg.triangular_solve(lower_tri, projected, left_side=False, lower=...  24.7 us
  transfers between devices with their start and end apart: 4, of which 4 were waited for; matrix products, arithmetic and copies ran while one was open for 0% of the time, Pallas kernels for 0%

profile of v1, /device:TPU:1, one launch (start us, length us, event | category | flops | bytes accessed | tf_op | source)
XLA Modules:
  0.0 477.1 jit_solution(18086389481217033530)
XLA Ops:
  7.2 1.8 copy-done
  9.1 3.0 fusion.16
  12.1 133.1 %all-reduce.3.cloned.1.call-done = f32[2048,128]{1,0:T(8,128)} async-done(((f32[2048,128]{1,0:T(8,128)}), f32[2048,128]{1,0:T(8,128)}) %all-reduce.3.cloned.1.call-update) | async-done | bytes 1048592 | tf_op jit(solution)/shard_map/psum | solution.py:22
  145.2 2.4 convolution_multiply_fusion.1
  148.8 56.7 %all-gather.5.cloned.1.call-done = f32[4096,128]{1,0:T(8,128)} async-done(((f32[128,128]{1,0:T(8,128)}), f32[4096,128]{1,0:T(8,128)}) %all-gather.5.cloned.1.call-update) | async-done | bytes 2097168 | tf_op jit(solution)/shard_map/all_gather | solution.py:29
  205.4 2.3 reduce_sum.18
  207.8 1.6 copy.8
  209.3 1.5 fusion.9
  210.8 13.2 %cholesky.44 = f32[128,128]{1,0:T(8,128)} custom-call(f32[128,128]{1,0:T(8,128)} %fusion.9), custom_call_target="Cholesky" | custom-call | tf_op jit(solution)/shard_map/jit(cholesky)/cholesky | solution.py:33
  225.5 2.1 fusion.5
  227.7 11.3 %custom-call.6 = f32[1,128,128]{1,2,0:T(8,128)} custom-call(f32[1,128,128]{2,1,0:T(8,128)} %fusion.5), custom_call_target="InvertDiagBlocksLowerTriangular" | custom-call | tf_op jit(solution)/shard_map/triangular_solve/custom-call.0 | solution.py:34
  240.3 2.4 convolution_bitcast_fusion
  242.9 128.3 %all-reduce.5.cloned.1.call-done = f32[2048,128]{1,0:T(8,128)} async-done(((f32[2048,128]{1,0:T(8,128)}), f32[2048,128]{1,0:T(8,128)}) %all-reduce.5.cloned.1.call-update) | async-done | bytes 1048592 | tf_op jit(solution)/shard_map/psum | solution.py:22
  371.2 2.4 convolution_multiply_fusion
  374.8 56.7 %all-gather.7.cloned.1.call-done = f32[4096,128]{1,0:T(8,128)} async-done(((f32[128,128]{1,0:T(8,128)}), f32[4096,128]{1,0:T(8,128)}) %all-gather.7.cloned.1.call-update) | async-done | bytes 2097168 | tf_op jit(solution)/shard_map/all_gather | solution.py:29
  431.5 2.3 reduce_sum.19
  433.8 1.6 copy.9
  435.4 1.5 fusion.7
  436.9 13.2 %cholesky.55 = f32[128,128]{1,0:T(8,128)} custom-call(f32[128,128]{1,0:T(8,128)} %fusion.7), custom_call_target="Cholesky" | custom-call | tf_op jit(solution)/shard_map/jit(cholesky)/cholesky | solution.py:33
  451.6 2.1 fusion.13
  453.7 1.6 copy.11
  455.3 11.3 %custom-call.7 = f32[1,128,128]{1,2,0:T(8,128)} custom-call(f32[1,128,128]{2,1,0:T(8,128)} %get-tuple-element.9), custom_call_target="InvertDiagBlocksLowerTriangular" | custom-call | tf_op jit(solution)/shard_map/triangular_solve/custom-call.0 | solution.py:34
  466.6 2.1 convolution_bitcast_fusion.1
  468.7 1.9 copy.10
  (16 shorter events, 7.0 us)
Async XLA Ops:
  7.2 1.9 copy-start
  7.2 138.0 %all-reduce.3.cloned.1.call-start = ((), (), s32[]{:S(2)}) async-start(), calls=%async_computation | async-start | bytes 2097152 | tf_op jit(solution)/shard_map/psum | solution.py:22
  12.1 193.4 %all-gather.5.cloned.1.call-start = ((), (), s32[]{:S(2)}) async-start(), calls=%async_computation.2 | async-start | bytes 2162688 | tf_op jit(solution)/shard_map/all_gather | solution.py:29
  148.7 222.5 %all-reduce.5.cloned.1.call-start = ((), (), s32[]{:S(2)}) async-start(), calls=%async_computation.1 | async-start | bytes 2097152 | tf_op jit(solution)/shard_map/psum | solution.py:22
  242.7 188.8 %all-gather.7.cloned.1.call-start = ((), (), s32[]{:S(2)}) async-start(), calls=%async_computation.3 | async-start | bytes 2162688 | tf_op jit(solution)/shard_map/all_gather | solution.py:29
Sparse Core Ops, SparseCore 0:
  13.2 131.9 all-reduce.2
  148.8 56.5 all-gather.4
  242.8 128.3 all-reduce.4
  374.9 56.5 all-gather.6

commit v2 on v0

--- a/solution.py
+++ b/solution.py
@@ -24,7 +24,8 @@
         projected = jnp.dot(outcomes, day_weights, preferred_element_type=jnp.float32)
         projected = projected / math.sqrt(day_count)
         gram_local = jnp.dot(projected.T, projected, precision=lax.Precision.HIGHEST) / unit_count
-        gram = lax.psum(gram_local, ("gx", "gy", "gz"))
+        y = lax.psum(gram_local, ("gy", "gz"))
+        gram = lax.psum(y, "gx")
         lower_tri = jnp.linalg.cholesky(gram)
         left_basis = lax.linalg.triangular_solve(
             lower_tri, projected, left_side=False, lower=True, transpose_a=True

time: 608 us -> 569 us (0.936)
  waiting for transfers between devices: 510 us -> 468 us
    psum x2 -> x4, waiting for transfers between devices: 247 us -> 203 us  [the longest x2 135 us: per_device(): y = lax.psum(gram_local, ('gy', 'gz'))]
  transfers between devices with their start and end apart: 4 -> 6, of which waited for: 4 -> 6; matrix products, arithmetic and copies ran while one was open for 0% -> 0% of each run, Pallas kernels for 0% -> 0%
where the time goes in v2:
time: 569 us; the launch traced here: 566 us
  waiting for transfers between devices  468 us (82%)
  other arithmetic  59.2 us (10%)
  matrix products  15.8 us (3%)
  between operations  14.1 us (2%)
  local copies, waits for them, and re-layouts  8.45 us (1%)
    psum x2, waiting for transfers between devices, per_device(): summed = lax.psum(partial_sum, ('gx', 'gy', 'gz'))  264 us
    psum x2, waiting for transfers between devices, per_device(): y = lax.psum(gram_local, ('gy', 'gz'))  135 us
    psum x2, waiting for transfers between devices, per_device(): gram = lax.psum(y, 'gx')  68.2 us
    another operation x6, other arithmetic, per_device(): lower_tri = jnp.linalg.cholesky(gram)  29.4 us
    another operation x3, other arithmetic, per_device(): lax.linalg.triangular_solve(lower_tri, projected, left_side=False, lower=...  24.7 us
  transfers between devices with their start and end apart: 6, of which 6 were waited for; matrix products, arithmetic and copies ran while one was open for 0% of the time, Pallas kernels for 0%

profile of v2, /device:TPU:1, one launch (start us, length us, event | category | flops | bytes accessed | tf_op | source)
XLA Modules:
  0.0 565.8 jit_solution(15883863701231694764)
XLA Ops:
  7.2 1.8 copy-done
  9.1 3.0 fusion.16
  12.1 133.1 %all-reduce.7.cloned.1.call-done = f32[2048,128]{1,0:T(8,128)} async-done(((f32[2048,128]{1,0:T(8,128)}), f32[2048,128]{1,0:T(8,128)}) %all-reduce.7.cloned.1.call-update) | async-done | bytes 1048592 | tf_op jit(solution)/shard_map/psum | solution.py:22
  145.2 2.4 convolution_multiply_fusion.1
  148.8 67.6 %all-reduce.9.cloned.1.call-done = f32[128,128]{0,1:T(8,128)} async-done(((f32[128,128]{0,1:T(8,128)}), f32[128,128]{0,1:T(8,128)}) %all-reduce.9.cloned.1.call-update) | async-done | bytes 65552 | tf_op jit(solution)/shard_map/psum | solution.py:27
  216.5 34.1 %all-reduce.11.cloned.1.call-done = f32[128,128]{0,1:T(8,128)} async-done(((f32[128,128]{0,1:T(8,128)}), f32[128,128]{0,1:T(8,128)}) %all-reduce.11.cloned.1.call-update) | async-done | bytes 65552 | tf_op jit(solution)/shard_map/psum | solution.py:28
  250.6 1.6 copy.5
  252.2 1.5 fusion.9
  253.7 13.2 %cholesky.44 = f32[128,128]{1,0:T(8,128)} custom-call(f32[128,128]{1,0:T(8,128)} %fusion.9), custom_call_target="Cholesky" | custom-call | tf_op jit(solution)/shard_map/jit(cholesky)/cholesky | solution.py:29
  268.4 2.1 fusion.5
  270.5 11.3 %custom-call.6 = f32[1,128,128]{1,2,0:T(8,128)} custom-call(f32[1,128,128]{2,1,0:T(8,128)} %fusion.5), custom_call_target="InvertDiagBlocksLowerTriangular" | custom-call | tf_op jit(solution)/shard_map/triangular_solve/custom-call.0 | solution.py:30
  283.1 2.4 convolution_bitcast_fusion
  285.6 131.4 %all-reduce.13.cloned.1.call-done = f32[2048,128]{1,0:T(8,128)} async-done(((f32[2048,128]{1,0:T(8,128)}), f32[2048,128]{1,0:T(8,128)}) %all-reduce.13.cloned.1.call-update) | async-done | bytes 1048592 | tf_op jit(solution)/shard_map/psum | solution.py:22
  417.0 2.4 convolution_multiply_fusion
  420.8 67.3 %all-reduce.15.cloned.1.call-done = f32[128,128]{0,1:T(8,128)} async-done(((f32[128,128]{0,1:T(8,128)}), f32[128,128]{0,1:T(8,128)}) %all-reduce.15.cloned.1.call-update) | async-done | bytes 65552 | tf_op jit(solution)/shard_map/psum | solution.py:27
  488.1 34.0 %all-reduce.17.cloned.1.call-done = f32[128,128]{0,1:T(8,128)} async-done(((f32[128,128]{0,1:T(8,128)}), f32[128,128]{0,1:T(8,128)}) %all-reduce.17.cloned.1.call-update) | async-done | bytes 65552 | tf_op jit(solution)/shard_map/psum | solution.py:28
  522.2 1.6 copy.7
  523.7 1.5 fusion.7
  525.2 13.2 %cholesky.55 = f32[128,128]{1,0:T(8,128)} custom-call(f32[128,128]{1,0:T(8,128)} %fusion.7), custom_call_target="Cholesky" | custom-call | tf_op jit(solution)/shard_map/jit(cholesky)/cholesky | solution.py:29
  539.9 2.1 fusion.13
  542.1 1.6 copy.9
  543.6 11.3 %custom-call.7 = f32[1,128,128]{1,2,0:T(8,128)} custom-call(f32[1,128,128]{2,1,0:T(8,128)} %get-tuple-element.7), custom_call_target="InvertDiagBlocksLowerTriangular" | custom-call | tf_op jit(solution)/shard_map/triangular_solve/custom-call.0 | solution.py:30
  554.9 2.1 convolution_bitcast_fusion.1
  557.0 1.9 copy.8
  (20 shorter events, 7.1 us)
Async XLA Ops:
  7.2 1.9 copy-start
  7.2 138.0 %all-reduce.7.cloned.1.call-start = ((), (), s32[]{:S(2)}) async-start(), calls=%async_computation | async-start | bytes 2097152 | tf_op jit(solution)/shard_map/psum | solution.py:22
  12.1 204.3 %all-reduce.9.cloned.1.call-start = ((), (), s32[]{:S(2)}) async-start(), calls=%async_computation.1 | async-start | bytes 131072 | tf_op jit(solution)/shard_map/psum | solution.py:27
  148.7 101.9 %all-reduce.11.cloned.1.call-start = ((), (), s32[]{:S(2)}) async-start(), calls=%async_computation.2 | async-start | bytes 131072 | tf_op jit(solution)/shard_map/psum | solution.py:28
  216.4 200.6 %all-reduce.13.cloned.1.call-start = ((), (), s32[]{:S(2)}) async-start(), calls=%async_computation.3 | async-start | bytes 2097152 | tf_op jit(solution)/shard_map/psum | solution.py:22
  285.5 202.6 %all-reduce.15.cloned.1.call-start = ((), (), s32[]{:S(2)}) async-start(), calls=%async_computation.4 | async-start | bytes 131072 | tf_op jit(solution)/shard_map/psum | solution.py:27
  420.6 101.6 %all-reduce.17.cloned.1.call-start = ((), (), s32[]{:S(2)}) async-start(), calls=%async_computation.5 | async-start | bytes 131072 | tf_op jit(solution)/shard_map/psum | solution.py:28
Sparse Core Ops, SparseCore 0:
  13.2 131.9 all-reduce.6
  149.1 67.1 all-reduce.8
  218.7 31.8 all-reduce.10
  285.7 131.3 all-reduce.12
  420.9 67.1 all-reduce.14
  490.3 31.8 all-reduce.16
